TPU v7x, 32 devices: a whole 2x2x4 slice. The times are simulated.
32 devices in a mesh: gz: 2 (over core), pa: 16 (over z, y, x).
Axes of the slice: x: 2, y: 2, z: 4, core: 2. Of those that a mesh axis runs over, the one named last changes fastest.
Arguments:
- velocity: float32 [3, 2, 2, 512, 1024], P(None, 'gz', None, 'pa'), may hold values from -3 to 3
- mode_mask: int32 [512, 1024], P('pa'), may hold values from 0 to 1, as said below
Outputs:
- velocity_next: float32 [3, 2, 2, 512, 1024], P(None, 'gz', None, 'pa')
- divergence: float32 [2, 2, 512, 1024], P('gz', None, 'pa')
Inputs may be any that keep to these rules, and one draw needn't show every extreme that they name: mode_mask is 1 exactly where |s(m)| <= A and n <= B, for one A from 256 to 340 and one B from 256 to 340 in each draw, and 0 elsewhere.
All inputs are finite; a program needn't handle non-finite values.
Results may differ from a plain program's by a relative error of at most 0.00005.
Values sent between devices are 32-bit elements; how exact they have to be, the bound alone decides.
A program may use at most 64 MiB of HBM per device.

v0:
```python
import functools
import math

import jax
import jax.numpy as jnp
import numpy as np
from jax import lax
from jax.experimental import pallas as pl
from jax.experimental.pallas import tpu as pltpu
from jax.sharding import PartitionSpec as P

precise = lax.Precision.HIGHEST
time_step = 0.2
viscosity = 0.25


def extended(block, sides, width):
    for axis, dim in sides:
        count = lax.axis_size(axis)
        forward = [(i, i + 1) for i in range(count - 1)]
        backward = [(target, source) for source, target in forward]
        low = lax.ppermute(
            lax.slice_in_dim(block, block.shape[dim] - width, None, axis=dim), axis, forward
        )
        high = lax.ppermute(lax.slice_in_dim(block, 0, width, axis=dim), axis, backward)
        block = jnp.concatenate([low, block, high], axis=dim)
    return block


def phase_pair(rows, cols, period, sign):
    angle = 2.0 * math.pi / period * (rows[:, None] * cols[None, :] % period).astype(jnp.float32)
    return (jnp.cos(angle), sign * jnp.sin(angle))


def factor_sizes(length):
    second = 2 ** ((length.bit_length() - 1) // 2)
    return (length // second, second)


def factored(real, imag, sign, first, second, keep):
    used = real.shape[-1] // second
    lead = real.shape[:-1]
    a_index = jnp.arange(used, dtype=jnp.int32)
    c_index = jnp.arange(first, dtype=jnp.int32)
    b_index = jnp.arange(second, dtype=jnp.int32)
    d_index = jnp.arange(keep, dtype=jnp.int32)
    one_cos, one_sin = phase_pair(a_index, c_index, first, sign)
    turn_cos, turn_sin = phase_pair(c_index, b_index, first * second, sign)
    two_cos, two_sin = phase_pair(b_index, d_index, second, sign)
    x_real = real.reshape(lead + (used, second))
    a_real = jnp.einsum("...ab,ac->...cb", x_real, one_cos, precision=precise)
    a_imag = jnp.einsum("...ab,ac->...cb", x_real, one_sin, precision=precise)
    if imag is not None:
        x_imag = imag.reshape(lead + (used, second))
        a_real = a_real - jnp.einsum("...ab,ac->...cb", x_imag, one_sin, precision=precise)
        a_imag = a_imag + jnp.einsum("...ab,ac->...cb", x_imag, one_cos, precision=precise)
    t_real = a_real * turn_cos - a_imag * turn_sin
    t_imag = a_real * turn_sin + a_imag * turn_cos
    o_real = jnp.einsum("...cb,bd->...dc", t_real, two_cos, precision=precise) - jnp.einsum(
        "...cb,bd->...dc", t_imag, two_sin, precision=precise
    )
    o_imag = jnp.einsum("...cb,bd->...dc", t_real, two_sin, precision=precise) + jnp.einsum(
        "...cb,bd->...dc", t_imag, two_cos, precision=precise
    )
    return (o_real.reshape(lead + (keep * first,)), o_imag.reshape(lead + (keep * first,)))


def wall_first(padded):
    return 0.5 * (padded[2:] - padded[:-2])


def times_wave(wave, field):
    return jnp.stack([-wave * field[:, 1], wave * field[:, 0]], 1)


def by_steps(velocity, mode_mask):
    groups = lax.axis_size("pa")
    rank = lax.axis_index("pa")
    depth = velocity.shape[1]
    kyl = velocity.shape[3]
    ncols = velocity.shape[4]
    lines = ncols // groups
    half = kyl * groups
    nrows = 2 * half
    x_first, x_second = factor_sizes(ncols)
    y_first, y_second = factor_sizes(nrows)
    x_scale = 1.0 / math.sqrt(ncols)
    y_scale = 1.0 / math.sqrt(nrows)
    modes = jnp.arange(ncols, dtype=jnp.int32)
    signed = jnp.where(modes < ncols // 2, modes, modes - ncols)
    kx_wave = 2.0 * math.pi / ncols * signed.astype(jnp.float32)
    own_modes = rank * kyl + jnp.arange(kyl, dtype=jnp.int32)
    ky_wave = (2.0 * math.pi / nrows * own_modes.astype(jnp.float32))[:, None]
    span_index = jnp.arange(half, dtype=jnp.int32)
    weight = jnp.where(span_index == 0, 1.0, 2.0).astype(jnp.float32)

    def to_modes(received):
        count = received.shape[0]
        planes = received.shape[1]
        blocks = received.reshape(count, planes, 2, groups, lines, kyl)
        blocks = jnp.transpose(blocks, (0, 1, 2, 5, 3, 4)).reshape(count, planes, 2, kyl, ncols)
        h_real, h_imag = factored(
            blocks[:, :, 0], blocks[:, :, 1], -1.0, x_first, x_second, x_second
        )
        return jnp.stack([h_real, h_imag], 2) * x_scale

    padded = extended(velocity, (("gz", 1),), 1)
    u_spec = velocity[0]
    v_spec = velocity[1]
    w_spec = velocity[2]
    omega_x = times_wave(ky_wave, w_spec) - wall_first(padded[1])
    omega_y = wall_first(padded[0]) - times_wave(kx_wave, w_spec)
    omega_z = times_wave(kx_wave, v_spec) - times_wave(ky_wave, u_spec)
    vorticity = jnp.stack([omega_x, omega_y, omega_z], 0)
    both = jnp.concatenate([velocity, vorticity], 0)
    count = both.shape[0]
    g_real, g_imag = factored(both[:, :, 0], both[:, :, 1], 1.0, x_first, x_second, x_second)
    joined = jnp.stack([g_real, g_imag], 2) * x_scale
    joined = jnp.swapaxes(joined, 3, 4)
    received = lax.all_to_all(
        joined.reshape(count, depth, 2, groups, lines * kyl),
        "pa",
        split_axis=3,
        concat_axis=3,
        tiled=True,
    )
    to_count = received.shape[0]
    planes = received.shape[1]
    blocks = received.reshape(to_count, planes, 2, groups, lines, kyl)
    blocks = jnp.transpose(blocks, (0, 1, 2, 4, 3, 5)).reshape(to_count, planes, 2, lines, half)
    blocks = blocks * weight
    p_real, p_imag = factored(blocks[:, :, 0], blocks[:, :, 1], 1.0, y_first, y_second, y_second)
    grid = p_real * y_scale
    speed_grid = grid[:3]
    swirl_grid = grid[3:]
    u_grid = speed_grid[0]
    v_grid = speed_grid[1]
    w_grid = speed_grid[2]
    cross = jnp.stack(
        [
            v_grid * swirl_grid[2] - w_grid * swirl_grid[1],
            w_grid * swirl_grid[0] - u_grid * swirl_grid[2],
            u_grid * swirl_grid[1] - v_grid * swirl_grid[0],
        ],
        0,
    )
    count = cross.shape[0]
    q_real, q_imag = factored(cross, None, -1.0, y_first, y_second, y_second // 2)
    joined = jnp.stack([q_real, q_imag], 2) * y_scale
    joined = joined.reshape(count, depth, 2, lines, groups, kyl)
    joined = jnp.transpose(joined, (0, 1, 2, 4, 3, 5))
    nonlinear = to_modes(
        lax.all_to_all(
            joined.reshape(count, depth, 2, groups, lines * kyl),
            "pa",
            split_axis=3,
            concat_axis=3,
            tiled=True,
        )
    )
    mask = mode_mask.astype(jnp.float32)
    viscous = padded[:, 2:] - 2.0 * padded[:, 1:-1] + padded[:, :-2]
    viscous = viscous - (kx_wave * kx_wave + ky_wave * ky_wave) * velocity
    following = velocity + time_step * (nonlinear * mask + viscosity * viscous)
    w_padded = extended(following[2], (("gz", 0),), 1)
    divergence = (
        times_wave(kx_wave, following[0]) + times_wave(ky_wave, following[1]) + wall_first(w_padded)
    )
    return (following, divergence)


LANES = 128


def split(value):
    high = value.astype(jnp.bfloat16)
    low = (value - high.astype(jnp.float32)).astype(jnp.bfloat16)
    return high, low


def dot3(left, right):
    def dot(a, b):
        return jnp.dot(a, b, preferred_element_type=jnp.float32)

    return dot(left[0], right[0]) + (dot(left[0], right[1]) + dot(left[1], right[0]))


def turned(z, k, n, sign):
    real, imag = z
    if k == 0:
        return z
    if 4 * k == n:
        return (-imag, real) if sign > 0 else (imag, -real)
    c = math.cos(2.0 * math.pi * k / n)
    s = sign * math.sin(2.0 * math.pi * k / n)
    return (real * c - imag * s, real * s + imag * c)


def short_fft(z, sign):
    n = len(z)
    if n == 1:
        return z
    even = short_fft(z[0::2], sign)
    odd = short_fft(z[1::2], sign)
    low, high = [], []
    for k in range(n // 2):
        t = turned(odd[k], k, n, sign)
        low.append((even[k][0] + t[0], even[k][1] + t[1]))
        high.append((even[k][0] - t[0], even[k][1] - t[1]))
    return low + high


@functools.lru_cache(None)
def tables(ncols, nrows, lines):
    radix = ncols // LANES
    quarter = nrows // 4
    b = np.arange(LANES)
    angle = 2.0 * np.pi * (np.outer(b, b) % LANES) / LANES
    c, s = np.cos(angle), np.sin(angle)
    order = np.concatenate(
        [p * LANES + h * lines + np.arange(lines) for h in range(LANES // lines) for p in (0, 1)]
    )
    to_grid = np.block([[c, s], [-s, c]])[:, order] / math.sqrt(ncols)
    to_wave = np.block([[c, -s], [s, c]])[order, :] / math.sqrt(ncols) / 2.0
    q = np.arange(quarter)
    angle = 2.0 * np.pi * (np.outer(q, q) % quarter) / quarter
    span = np.concatenate([np.cos(angle), -np.sin(angle)], 1) * (2.0 / math.sqrt(nrows))
    angle = 2.0 * np.pi * np.outer(q, np.arange(4)) / nrows
    span_turn = np.concatenate([np.cos(angle), np.sin(angle)], 1)
    angle = 2.0 * np.pi * np.outer(np.arange(radix), b) / ncols
    line_turn = np.concatenate([np.cos(angle), np.sin(angle)], 0)
    return [np.asarray(t, np.float32) for t in (to_grid, to_wave, span, span_turn, line_turn)]


def kernel(
    groups, kept,
    vel_hbm, mask_hbm, to_grid_hbm, to_wave_hbm, span_hbm, span_turn_hbm, line_turn_hbm, kx_hbm,
    out_hbm, div_hbm,
    vel, mask, to_grid, to_wave, span, span_turn, line_turn, kx_ref, out, div,
    send, recv, vel_other, g_other, q_send, q_recv, w_other, grid,
    load_sem, store_sem, send_sem, recv_sem, q_send_sem, q_recv_sem, local_sem, pair_sem, pair_recv_sem,
):
    me = lax.axis_index("pa")
    side = lax.axis_index("gz")
    partner = {"gz": 1 - side}
    kyl = vel.shape[3]
    ncols = vel.shape[4]
    lines = ncols // groups
    half = kyl * groups
    nrows = 2 * half
    quarter = half // 2
    radix = ncols // LANES
    dz = jnp.where(side == 0, 0.5, -0.5).astype(jnp.float32)

    loads = {}
    for index, (name, src, dst) in enumerate(
        (
            ("v", vel_hbm.at[1], vel.at[1]),
            ("to_grid", to_grid_hbm, to_grid),
            ("line_turn", line_turn_hbm, line_turn),
            ("u", vel_hbm.at[0], vel.at[0]),
            ("w", vel_hbm.at[2], vel.at[2]),
            ("kx", kx_hbm, kx_ref),
            ("span", span_hbm, span),
            ("span_turn", span_turn_hbm, span_turn),
            ("to_wave", to_wave_hbm, to_wave),
            ("mask", mask_hbm, mask),
        )
    ):
        loads[name] = pltpu.make_async_copy(src, dst, load_sem.at[index])
        loads[name].start()
    stores = [pltpu.make_async_copy(out.at[f], out_hbm.at[f], store_sem.at[f]) for f in range(3)]
    stores.append(pltpu.make_async_copy(div, div_hbm, store_sem.at[3]))

    barrier = pltpu.get_barrier_semaphore()

    @pl.loop(1, groups)
    def _(k):
        pl.semaphore_signal(barrier, inc=1, device_id={"pa": lax.rem(me + k, groups)})

    pl.semaphore_signal(barrier, inc=1, device_id=partner)

    own_n = me * kyl + lax.broadcasted_iota(jnp.int32, (kyl, LANES), 0)
    ky_own = 2.0 * math.pi / nrows * own_n.astype(jnp.float32)
    weight = jnp.where(own_n == 0, 0.5, 1.0).astype(jnp.float32)
    loads["v"].wait()
    loads["to_grid"].wait()
    loads["line_turn"].wait()
    grid_w = split(to_grid[...])

    def block(ref, a):
        return ref[:, a * LANES : (a + 1) * LANES]

    def kx_at(a):
        return jnp.broadcast_to(kx_ref[:, a * LANES : (a + 1) * LANES], (kyl, LANES))

    def spec(comp, a):
        at = slice(a * LANES, (a + 1) * LANES)
        return (vel[comp, 0, 0, :, at], vel[comp, 0, 1, :, at])

    def x_forward(slot, z):
        z = [(r * weight, i * weight) for r, i in z]
        lhs = []
        for c, (r, i) in enumerate(short_fft(z, 1.0)):
            if c > 0:
                tc = jnp.broadcast_to(line_turn[c : c + 1, :], (kyl, LANES))
                ts = jnp.broadcast_to(line_turn[radix + c : radix + c + 1, :], (kyl, LANES))
                r, i = r * tc - i * ts, r * ts + i * tc
            lhs.append(jnp.concatenate([r, i], 1))
        res = dot3(split(jnp.concatenate(lhs, 0)), grid_w)
        for c in range(radix):
            rows = res[c * kyl : (c + 1) * kyl]
            send[slot, 2 * c] = rows[:, :LANES]
            send[slot, 2 * c + 1] = rows[:, LANES:]

    def field_copy(slot, dest, source):
        return pltpu.make_async_remote_copy(
            src_ref=send.at[slot, dest],
            dst_ref=recv.at[slot, source],
            send_sem=send_sem.at[slot, dest],
            recv_sem=recv_sem.at[slot, source],
            device_id={"pa": dest},
        )

    def own_copy(slot):
        return pltpu.make_async_copy(send.at[slot, me], recv.at[slot, me], local_sem.at[slot])

    def send_field(slot):
        @pl.loop(1, groups)
        def _(k):
            field_copy(slot, lax.rem(me + k, groups), me).start()

        own_copy(slot).start()

    def wait_field(slot):
        own_copy(slot).wait()

        @pl.loop(1, groups)
        def _(k):
            source = lax.rem(me + groups - k, groups)
            field_copy(slot, source, source).wait_recv()

    def pair_copy(index, src, dst):
        return pltpu.make_async_remote_copy(
            src_ref=src,
            dst_ref=dst,
            send_sem=pair_sem.at[index],
            recv_sem=pair_recv_sem.at[index],
            device_id=partner,
        )

    x_forward(0, [spec(1, a) for a in range(radix)])
    pl.semaphore_wait(barrier, groups)
    send_field(0)
    loads["u"].wait()
    loads["w"].wait()
    loads["kx"].wait()
    vel_copies = [pair_copy(f, vel.at[f, 0], vel_other.at[f]) for f in range(3)]
    for copy in vel_copies:
        copy.start()
    x_forward(1, [spec(0, a) for a in range(radix)])
    send_field(1)
    x_forward(2, [spec(2, a) for a in range(radix)])
    send_field(2)
    vel_copies[0].wait_recv()
    swirl = []
    for a in range(radix):
        w, kx = spec(2, a), kx_at(a)
        at = slice(a * LANES, (a + 1) * LANES)
        swirl.append((dz * vel_other[0, 0, :, at] + kx * w[1], dz * vel_other[0, 1, :, at] - kx * w[0]))
    x_forward(3, swirl)
    send_field(3)
    swirl = []
    for a in range(radix):
        v, u, kx = spec(1, a), spec(0, a), kx_at(a)
        swirl.append((ky_own * u[1] - kx * v[1], kx * v[0] - ky_own * u[0]))
    x_forward(4, swirl)
    send_field(4)

    vel_copies[1].wait_recv()
    vel_copies[2].wait_recv()
    ky_wide = ky_own[:, :1]
    square = kx_ref[...] * kx_ref[...] + ky_wide * ky_wide
    for f in range(3):
        for part in range(2):
            own = vel[f, 0, part]
            viscous = vel_other[f, part] - 2.0 * own - square * own
            out[f, 0, part] = time_step * viscosity * viscous

    loads["span"].wait()
    loads["span_turn"].wait()
    span_w = split(span[...])
    lane = lax.broadcasted_iota(jnp.int32, (half, LANES), 1)
    first = lane < lines
    all_n = lax.broadcasted_iota(jnp.int32, (half, LANES), 0)
    ky_all = 2.0 * math.pi / nrows * all_n.astype(jnp.float32)
    ky_all = jnp.where(first, -ky_all, ky_all)

    def swap(value):
        return pltpu.roll(value, lines, 1)

    def turn(t):
        c = jnp.broadcast_to(span_turn[:, t : t + 1], (quarter, LANES))
        s = jnp.broadcast_to(span_turn[:, 4 + t : 5 + t], (quarter, LANES))
        return c, s

    def field(slot):
        return recv[slot].reshape(half, LANES)

    def y_forward(pair, one, two):
        real = jnp.where(first, one, swap(two))
        imag = jnp.where(first, swap(one), two)
        rl, rh, il, ih = real[:quarter], real[quarter:], imag[:quarter], imag[quarter:]
        columns = []
        for t, (r, i) in enumerate(
            [(rl + rh, il + ih), (rl - ih, il + rh), (rl - rh, il - ih), (rl + ih, il - rh)]
        ):
            if t > 0:
                c, s = turn(t)
                r, i = r * c - i * s, r * s + i * c
            columns.append(jnp.concatenate([r, i], 0))
        res = dot3(span_w, split(jnp.concatenate(columns, 1)))
        for t in range(4):
            grid[pair, t] = res[:, t * LANES : (t + 1) * LANES]

    back_w = span[...]
    back_w = split(jnp.concatenate([back_w[:, :quarter], back_w[:, quarter:]], 0))
    lo = lax.broadcasted_iota(jnp.int32, (quarter, LANES), 1) < lines

    def q_copy(comp, dest, source):
        return pltpu.make_async_remote_copy(
            src_ref=q_send.at[comp, dest],
            dst_ref=q_recv.at[comp, source],
            send_sem=q_send_sem.at[comp, dest],
            recv_sem=q_recv_sem.at[comp, source],
            device_id={"pa": dest},
        )

    def q_own(comp):
        return pltpu.make_async_copy(q_send.at[comp, me], q_recv.at[comp, me], local_sem.at[5 + comp])

    def q_start(comp):
        @pl.loop(1, groups)
        def _(k):
            dest = lax.rem(me + k, groups)

            @pl.when(dest < kept)
            def _():
                q_copy(comp, dest, me).start()

        @pl.when(me < kept)
        def _():
            q_own(comp).start()

    def y_back(columns, comps):
        res = dot3(back_w, split(jnp.concatenate(columns, 1)))
        sums = []
        for t in range(4):
            r = res[:quarter, t * LANES : (t + 1) * LANES]
            i = res[quarter:, t * LANES : (t + 1) * LANES]
            if t > 0:
                c, s = turn(t)
                r, i = r * c + i * s, i * c - r * s
            sums.append((r, i))
        (r0, i0), (r1, i1), (r2, i2), (r3, i3) = sums
        low = (r0 + r1 + r2 + r3, i0 + i1 + i2 + i3)
        high = (r0 - r2 + (i1 - i3), i0 - i2 - (r1 - r3))
        for base, (r, i), count in (
            (0, low, quarter // kyl),
            (quarter // kyl, high, kept - quarter // kyl),
        ):
            rolled_i, rolled_r = swap(i), swap(r)
            packed = [jnp.where(lo, r, rolled_i), jnp.where(lo, rolled_r, i)]
            for comp, value in zip(comps, packed):
                q_send[comp, base : base + count] = value[: count * kyl].reshape(count, kyl, LANES)

    wait_field(0)
    v_copy = pair_copy(3, recv.at[0], g_other)
    v_copy.start()
    wait_field(1)
    y_forward(0, field(1), field(0))
    wait_field(2)
    v_copy.wait_recv()
    swirl_x = ky_all * swap(field(2)) - dz * g_other[...].reshape(half, LANES)
    wait_field(3)
    y_forward(1, field(3), swirl_x)
    columns = []
    for t in range(4):
        product = grid[0, t] * grid[1, t]
        columns.append(product - swap(product))
    y_back(columns, (2,))
    q_start(2)
    wait_field(4)
    y_forward(2, field(2), field(4))
    columns = []
    for t in range(4):
        speed, swirls, mixed = grid[0, t], grid[1, t], grid[2, t]
        x_part = swap(speed * mixed) - mixed * swirls
        y_part = mixed * swap(swirls) - speed * swap(mixed)
        columns.append(jnp.where(lo, x_part, swap(y_part)))
    y_back(columns, (0, 1))
    q_start(0)
    q_start(1)

    loads["to_wave"].wait()
    loads["mask"].wait()
    wave_w = split(to_wave[...])

    def x_back(comp):
        @pl.when(me < kept)
        def _():
            q_own(comp).wait()

            @pl.loop(1, groups)
            def _(k):
                source = lax.rem(me + groups - k, groups)
                q_copy(comp, source, source).wait_recv()

            rows = [
                jnp.concatenate([q_recv[comp, 2 * c], q_recv[comp, 2 * c + 1]], 1)
                for c in range(radix)
            ]
            res = dot3(split(jnp.concatenate(rows, 0)), wave_w)
            z = []
            for c in range(radix):
                r = res[c * kyl : (c + 1) * kyl, :LANES]
                i = res[c * kyl : (c + 1) * kyl, LANES:]
                if c > 0:
                    tc = jnp.broadcast_to(line_turn[c : c + 1, :], (kyl, LANES))
                    ts = jnp.broadcast_to(line_turn[radix + c : radix + c + 1, :], (kyl, LANES))
                    r, i = r * tc + i * ts, i * tc - r * ts
                z.append((r, i))
            for a, values in enumerate(short_fft(z, -1.0)):
                at = slice(a * LANES, (a + 1) * LANES)
                gain = time_step * mask[:, at].astype(jnp.float32)
                for part in range(2):
                    out[comp, 0, part, :, at] = out[comp, 0, part, :, at] + gain * values[part]

    x_back(2)
    w_copy = pair_copy(4, out.at[2, 0], w_other)
    w_copy.start()
    stores[2].start()
    x_back(0)
    stores[0].start()
    x_back(1)
    stores[1].start()
    kx_all = kx_ref[...]
    w_copy.wait_recv()
    for part, sign in ((0, -1.0), (1, 1.0)):
        u_next = vel[0, 0, 1 - part] + out[0, 0, 1 - part]
        v_next = vel[1, 0, 1 - part] + out[1, 0, 1 - part]
        w_next = vel_other[2, part] + w_other[part]
        div[0, part] = dz * w_next + sign * (kx_all * u_next + ky_wide * v_next)

    stores[3].start()
    for copy in stores:
        copy.wait()
    for copy in vel_copies + [v_copy, w_copy]:
        copy.wait_send()

    for slot in range(5):

        @pl.loop(1, groups)
        def _(k):
            field_copy(slot, lax.rem(me + k, groups), me).wait_send()

    for comp in range(3):

        @pl.loop(1, groups)
        def _(k):
            dest = lax.rem(me + k, groups)

            @pl.when(dest < kept)
            def _():
                q_copy(comp, dest, me).wait_send()


def in_one_kernel(velocity, mode_mask):
    groups = lax.axis_size("pa")
    kyl = velocity.shape[3]
    ncols = velocity.shape[4]
    lines = ncols // groups
    half = kyl * groups
    nrows = 2 * half
    kept = -(-(nrows // 3) // kyl)
    signed = np.where(np.arange(ncols) < ncols // 2, np.arange(ncols), np.arange(ncols) - ncols)
    kx = (np.float32(2.0 * math.pi / ncols) * signed.astype(np.float32))[None, :]
    operands = [velocity, mode_mask] + [jnp.asarray(t) for t in tables(ncols, nrows, lines)]
    operands.append(jnp.asarray(kx))
    f32 = jnp.float32
    whole = pl.BlockSpec(memory_space=pl.ANY)
    dma = pltpu.SemaphoreType.DMA
    change, divergence = pl.pallas_call(
        functools.partial(kernel, groups, kept),
        out_shape=(
            jax.ShapeDtypeStruct(velocity.shape, f32),
            jax.ShapeDtypeStruct(velocity.shape[1:], f32),
        ),
        in_specs=[pl.BlockSpec(memory_space=pltpu.HBM)] * len(operands),
        out_specs=(whole, whole),
        scratch_shapes=[pltpu.VMEM(t.shape, t.dtype) for t in operands]
        + [
            pltpu.VMEM(velocity.shape, f32),
            pltpu.VMEM(velocity.shape[1:], f32),
            pltpu.VMEM((5, groups, kyl, LANES), f32),
            pltpu.VMEM((5, groups, kyl, LANES), f32),
            pltpu.VMEM((3, 2, kyl, ncols), f32),
            pltpu.VMEM((groups, kyl, LANES), f32),
            pltpu.VMEM((3, groups, kyl, LANES), f32),
            pltpu.VMEM((3, groups, kyl, LANES), f32),
            pltpu.VMEM((2, kyl, ncols), f32),
            pltpu.VMEM((3, 4, half // 2, LANES), f32),
            dma((10,)),
            dma((4,)),
            dma((5, groups)),
            dma((5, groups)),
            dma((3, groups)),
            dma((3, groups)),
            dma((8,)),
            dma((5,)),
            dma((5,)),
        ],
        compiler_params=pltpu.CompilerParams(collective_id=0, has_side_effects=True, vmem_limit_bytes=32 * 2**20),
    )(*[pltpu.with_memory_space_constraint(x, pltpu.HBM) for x in operands])
    return velocity + change, divergence


def on_device(velocity, mode_mask):
    groups = lax.axis_size("pa")
    kyl = velocity.shape[3]
    ncols = velocity.shape[4]
    fits = (
        lax.axis_size("gz") == 2
        and velocity.shape[1] == 1
        and kyl % 8 == 0
        and 2 * (ncols // groups) == LANES
        and (kyl * groups // 2) % LANES == 0
        and ncols % LANES == 0
        and nrows_cover(kyl * groups)
    )
    return in_one_kernel(velocity, mode_mask) if fits else by_steps(velocity, mode_mask)


def nrows_cover(half):
    return 2 * half // 3 > half // 2


def solution(mesh):
    placed = (P(None, "gz", None, "pa", None), P("pa", None))
    return jax.shard_map(
        on_device,
        mesh=mesh,
        in_specs=placed,
        out_specs=(P(None, "gz", None, "pa", None), P("gz", None, "pa", None)),
        check_vma=False,
    )
```

profile of v0, /device:TPU:0, one launch (start us, length us, event | category | flops | bytes accessed | tf_op | source)
XLA Modules:
  0.0 60.0 jit_solution(9087809055294127944)
XLA Ops:
  0.6 0.0 copy-start
  0.6 57.6 %shard_map.95 = (f32[3,1,2,32,1024]{4,3,2,1,0:T(8,128)S(1)}, f32[1,2,32,1024]{3,2,1,0:T(8,128)S(1)}) custom-call(f32[3,1,2,32,1024]{4,3,2,1,0:T(8,128)} %vel_hbm.1, s32[32,1024]{1,0:T(8,128)} %mask_hbm.1, f32[256,256]{1,0:T(8,128)} %constant.12.clone.to_grid_hbm, f32[256,256]{1,0:T(8,128)} %constant.13.clone.to_wave_hbm, ...), custom_call_target="tpu_custom_call" | custom-call | tf_op jit(solution)/shard_map/pallas_call | solution.py:593
  58.3 0.0 copy-done
  58.3 1.0 %add.3 = f32[3,1,2,32,1024]{4,3,2,1,0:T(8,128)} add(f32[3,1,2,32,1024]{4,3,2,1,0:T(8,128)S(1)} %copy-done, f32[3,1,2,32,1024]{4,3,2,1,0:T(8,128)S(1)} %get-tuple-element.4) | non-fusion elementwise | flops 196608 | bytes 2359296 | tf_op jit(solution)/shard_map/add | solution.py:625
  59.3 0.7 %copy.11 = f32[1,2,32,1024]{3,2,1,0:T(8,128)} copy(f32[1,2,32,1024]{3,2,1,0:T(8,128)S(1)} %get-tuple-element.9) | data formatting | bytes 524288
Async XLA Ops:
  0.6 57.6 %copy-start = (f32[3,1,2,32,1024]{4,3,2,1,0:T(8,128)S(1)}, f32[3,1,2,32,1024]{4,3,2,1,0:T(8,128)}, u32[]{:S(2)}) copy-start(f32[3,1,2,32,1024]{4,3,2,1,0:T(8,128)} %vel_hbm.1) | copy-start | bytes 2359300
where the time goes:
time: 60.1 us; the launch traced here: 60 us
  Pallas kernels  57.6 us (96%)
  other arithmetic  1 us (2%)
  local copies, waits for them, and re-layouts  0.71 us (1%)
  between operations  0.65 us (1%)
    pallas_call x1, Pallas kernels, in_one_kernel(): pl.pallas_call(functools.partial(kernel, groups, kept), out_shape=(jax.Sh...  57.6 us

commit v1 on v0

--- a/solution.py
+++ b/solution.py
@@ -232,13 +232,17 @@
     return [np.asarray(t, np.float32) for t in (to_grid, to_wave, span, span_turn, line_turn)]
 
 
+field_batches = ((0, 2), (2, 2), (4, 1))
+back_batches = ((0, 1), (1, 2))
+
+
 def kernel(
     groups, kept,
     vel_hbm, mask_hbm, to_grid_hbm, to_wave_hbm, span_hbm, span_turn_hbm, line_turn_hbm, kx_hbm,
-    out_hbm, div_hbm,
-    vel, mask, to_grid, to_wave, span, span_turn, line_turn, kx_ref, out, div,
+    out, div,
+    vel, mask, to_grid, to_wave, span, span_turn, line_turn, kx_ref,
     send, recv, vel_other, g_other, q_send, q_recv, w_other, grid,
-    load_sem, store_sem, send_sem, recv_sem, q_send_sem, q_recv_sem, local_sem, pair_sem, pair_recv_sem,
+    load_sem, send_sem, recv_sem, q_send_sem, q_recv_sem, pair_sem, pair_recv_sem,
 ):
     me = lax.axis_index("pa")
     side = lax.axis_index("gz")
@@ -269,8 +273,6 @@
     ):
         loads[name] = pltpu.make_async_copy(src, dst, load_sem.at[index])
         loads[name].start()
-    stores = [pltpu.make_async_copy(out.at[f], out_hbm.at[f], store_sem.at[f]) for f in range(3)]
-    stores.append(pltpu.make_async_copy(div, div_hbm, store_sem.at[3]))
 
     barrier = pltpu.get_barrier_semaphore()
 
@@ -310,35 +312,33 @@
         res = dot3(split(jnp.concatenate(lhs, 0)), grid_w)
         for c in range(radix):
             rows = res[c * kyl : (c + 1) * kyl]
-            send[slot, 2 * c] = rows[:, :LANES]
-            send[slot, 2 * c + 1] = rows[:, LANES:]
-
-    def field_copy(slot, dest, source):
+            send[2 * c, slot] = rows[:, :LANES]
+            send[2 * c + 1, slot] = rows[:, LANES:]
+
+    def batch_copy(batch, dest, source):
+        slots = pl.ds(*field_batches[batch])
         return pltpu.make_async_remote_copy(
-            src_ref=send.at[slot, dest],
-            dst_ref=recv.at[slot, source],
-            send_sem=send_sem.at[slot, dest],
-            recv_sem=recv_sem.at[slot, source],
+            src_ref=send.at[dest, slots],
+            dst_ref=recv.at[source, slots],
+            send_sem=send_sem.at[batch, dest],
+            recv_sem=recv_sem.at[batch, source],
             device_id={"pa": dest},
         )
 
-    def own_copy(slot):
-        return pltpu.make_async_copy(send.at[slot, me], recv.at[slot, me], local_sem.at[slot])
-
-    def send_field(slot):
+    def send_batch(batch):
         @pl.loop(1, groups)
         def _(k):
-            field_copy(slot, lax.rem(me + k, groups), me).start()
-
-        own_copy(slot).start()
-
-    def wait_field(slot):
-        own_copy(slot).wait()
-
+            batch_copy(batch, lax.rem(me + k, groups), me).start()
+
+        first_slot, count = field_batches[batch]
+        for slot in range(first_slot, first_slot + count):
+            recv[me, slot] = send[me, slot]
+
+    def wait_batch(batch):
         @pl.loop(1, groups)
         def _(k):
             source = lax.rem(me + groups - k, groups)
-            field_copy(slot, source, source).wait_recv()
+            batch_copy(batch, source, source).wait_recv()
 
     def pair_copy(index, src, dst):
         return pltpu.make_async_remote_copy(
@@ -350,18 +350,16 @@
         )
 
     x_forward(0, [spec(1, a) for a in range(radix)])
-    pl.semaphore_wait(barrier, groups)
-    send_field(0)
     loads["u"].wait()
+    x_forward(1, [spec(0, a) for a in range(radix)])
     loads["w"].wait()
     loads["kx"].wait()
+    pl.semaphore_wait(barrier, groups)
+    send_batch(0)
     vel_copies = [pair_copy(f, vel.at[f, 0], vel_other.at[f]) for f in range(3)]
     for copy in vel_copies:
         copy.start()
-    x_forward(1, [spec(0, a) for a in range(radix)])
-    send_field(1)
     x_forward(2, [spec(2, a) for a in range(radix)])
-    send_field(2)
     vel_copies[0].wait_recv()
     swirl = []
     for a in range(radix):
@@ -369,13 +367,13 @@
         at = slice(a * LANES, (a + 1) * LANES)
         swirl.append((dz * vel_other[0, 0, :, at] + kx * w[1], dz * vel_other[0, 1, :, at] - kx * w[0]))
     x_forward(3, swirl)
-    send_field(3)
+    send_batch(1)
     swirl = []
     for a in range(radix):
         v, u, kx = spec(1, a), spec(0, a), kx_at(a)
         swirl.append((ky_own * u[1] - kx * v[1], kx * v[0] - ky_own * u[0]))
     x_forward(4, swirl)
-    send_field(4)
+    send_batch(2)
 
     vel_copies[1].wait_recv()
     vel_copies[2].wait_recv()
@@ -385,7 +383,7 @@
         for part in range(2):
             own = vel[f, 0, part]
             viscous = vel_other[f, part] - 2.0 * own - square * own
-            out[f, 0, part] = time_step * viscosity * viscous
+            out[f, 0, part] = own + time_step * viscosity * viscous
 
     loads["span"].wait()
     loads["span_turn"].wait()
@@ -405,7 +403,7 @@
         return c, s
 
     def field(slot):
-        return recv[slot].reshape(half, LANES)
+        return recv[:, slot].reshape(half, LANES)
 
     def y_forward(pair, one, two):
         real = jnp.where(first, one, swap(two))
@@ -427,30 +425,34 @@
     back_w = split(jnp.concatenate([back_w[:, :quarter], back_w[:, quarter:]], 0))
     lo = lax.broadcasted_iota(jnp.int32, (quarter, LANES), 1) < lines
 
-    def q_copy(comp, dest, source):
+    def q_copy(batch, dest, source):
+        slots = pl.ds(*back_batches[batch])
         return pltpu.make_async_remote_copy(
-            src_ref=q_send.at[comp, dest],
-            dst_ref=q_recv.at[comp, source],
-            send_sem=q_send_sem.at[comp, dest],
-            recv_sem=q_recv_sem.at[comp, source],
+            src_ref=q_send.at[dest, slots],
+            dst_ref=q_recv.at[source, slots],
+            send_sem=q_send_sem.at[batch, dest],
+            recv_sem=q_recv_sem.at[batch, source],
             device_id={"pa": dest},
         )
 
-    def q_own(comp):
-        return pltpu.make_async_copy(q_send.at[comp, me], q_recv.at[comp, me], local_sem.at[5 + comp])
-
-    def q_start(comp):
+    def q_start(batch):
         @pl.loop(1, groups)
         def _(k):
             dest = lax.rem(me + k, groups)
 
             @pl.when(dest < kept)
             def _():
-                q_copy(comp, dest, me).start()
-
-        @pl.when(me < kept)
-        def _():
-            q_own(comp).start()
+                q_copy(batch, dest, me).start()
+
+        first_slot, count = back_batches[batch]
+        for slot in range(first_slot, first_slot + count):
+            q_recv[me, slot] = q_send[me, slot]
+
+    def q_wait(batch):
+        @pl.loop(1, groups)
+        def _(k):
+            source = lax.rem(me + groups - k, groups)
+            q_copy(batch, source, source).wait_recv()
 
     def y_back(columns, comps):
         res = dot3(back_w, split(jnp.concatenate(columns, 1)))
@@ -472,25 +474,23 @@
             rolled_i, rolled_r = swap(i), swap(r)
             packed = [jnp.where(lo, r, rolled_i), jnp.where(lo, rolled_r, i)]
             for comp, value in zip(comps, packed):
-                q_send[comp, base : base + count] = value[: count * kyl].reshape(count, kyl, LANES)
-
-    wait_field(0)
-    v_copy = pair_copy(3, recv.at[0], g_other)
+                q_send[base : base + count, comp] = value[: count * kyl].reshape(count, kyl, LANES)
+
+    wait_batch(0)
+    v_copy = pair_copy(3, recv.at[:, 0], g_other)
     v_copy.start()
-    wait_field(1)
     y_forward(0, field(1), field(0))
-    wait_field(2)
+    wait_batch(1)
     v_copy.wait_recv()
     swirl_x = ky_all * swap(field(2)) - dz * g_other[...].reshape(half, LANES)
-    wait_field(3)
     y_forward(1, field(3), swirl_x)
     columns = []
     for t in range(4):
         product = grid[0, t] * grid[1, t]
         columns.append(product - swap(product))
-    y_back(columns, (2,))
-    q_start(2)
-    wait_field(4)
+    y_back(columns, (0,))
+    q_start(0)
+    wait_batch(2)
     y_forward(2, field(2), field(4))
     columns = []
     for t in range(4):
@@ -498,73 +498,65 @@
         x_part = swap(speed * mixed) - mixed * swirls
         y_part = mixed * swap(swirls) - speed * swap(mixed)
         columns.append(jnp.where(lo, x_part, swap(y_part)))
-    y_back(columns, (0, 1))
-    q_start(0)
+    y_back(columns, (1, 2))
     q_start(1)
 
     loads["to_wave"].wait()
     loads["mask"].wait()
     wave_w = split(to_wave[...])
 
-    def x_back(comp):
-        @pl.when(me < kept)
-        def _():
-            q_own(comp).wait()
-
-            @pl.loop(1, groups)
-            def _(k):
-                source = lax.rem(me + groups - k, groups)
-                q_copy(comp, source, source).wait_recv()
-
-            rows = [
-                jnp.concatenate([q_recv[comp, 2 * c], q_recv[comp, 2 * c + 1]], 1)
-                for c in range(radix)
-            ]
-            res = dot3(split(jnp.concatenate(rows, 0)), wave_w)
-            z = []
-            for c in range(radix):
-                r = res[c * kyl : (c + 1) * kyl, :LANES]
-                i = res[c * kyl : (c + 1) * kyl, LANES:]
-                if c > 0:
-                    tc = jnp.broadcast_to(line_turn[c : c + 1, :], (kyl, LANES))
-                    ts = jnp.broadcast_to(line_turn[radix + c : radix + c + 1, :], (kyl, LANES))
-                    r, i = r * tc + i * ts, i * tc - r * ts
-                z.append((r, i))
-            for a, values in enumerate(short_fft(z, -1.0)):
-                at = slice(a * LANES, (a + 1) * LANES)
-                gain = time_step * mask[:, at].astype(jnp.float32)
-                for part in range(2):
-                    out[comp, 0, part, :, at] = out[comp, 0, part, :, at] + gain * values[part]
-
-    x_back(2)
+    def x_back(slot, comp):
+        rows = [
+            jnp.concatenate([q_recv[2 * c, slot], q_recv[2 * c + 1, slot]], 1)
+            for c in range(radix)
+        ]
+        res = dot3(split(jnp.concatenate(rows, 0)), wave_w)
+        z = []
+        for c in range(radix):
+            r = res[c * kyl : (c + 1) * kyl, :LANES]
+            i = res[c * kyl : (c + 1) * kyl, LANES:]
+            if c > 0:
+                tc = jnp.broadcast_to(line_turn[c : c + 1, :], (kyl, LANES))
+                ts = jnp.broadcast_to(line_turn[radix + c : radix + c + 1, :], (kyl, LANES))
+                r, i = r * tc + i * ts, i * tc - r * ts
+            z.append((r, i))
+        for a, values in enumerate(short_fft(z, -1.0)):
+            at = slice(a * LANES, (a + 1) * LANES)
+            gain = time_step * mask[:, at].astype(jnp.float32)
+            for part in range(2):
+                out[comp, 0, part, :, at] = out[comp, 0, part, :, at] + gain * values[part]
+
+    @pl.when(me < kept)
+    def _():
+        q_wait(0)
+        x_back(0, 2)
+
     w_copy = pair_copy(4, out.at[2, 0], w_other)
     w_copy.start()
-    stores[2].start()
-    x_back(0)
-    stores[0].start()
-    x_back(1)
-    stores[1].start()
+
+    @pl.when(me < kept)
+    def _():
+        q_wait(1)
+        x_back(1, 0)
+        x_back(2, 1)
+
     kx_all = kx_ref[...]
     w_copy.wait_recv()
     for part, sign in ((0, -1.0), (1, 1.0)):
-        u_next = vel[0, 0, 1 - part] + out[0, 0, 1 - part]
-        v_next = vel[1, 0, 1 - part] + out[1, 0, 1 - part]
-        w_next = vel_other[2, part] + w_other[part]
-        div[0, part] = dz * w_next + sign * (kx_all * u_next + ky_wide * v_next)
-
-    stores[3].start()
-    for copy in stores:
-        copy.wait()
+        u_next = out[0, 0, 1 - part]
+        v_next = out[1, 0, 1 - part]
+        div[0, part] = dz * w_other[part] + sign * (kx_all * u_next + ky_wide * v_next)
+
     for copy in vel_copies + [v_copy, w_copy]:
         copy.wait_send()
 
-    for slot in range(5):
+    for batch in range(len(field_batches)):
 
         @pl.loop(1, groups)
         def _(k):
-            field_copy(slot, lax.rem(me + k, groups), me).wait_send()
-
-    for comp in range(3):
+            batch_copy(batch, lax.rem(me + k, groups), me).wait_send()
+
+    for batch in range(len(back_batches)):
 
         @pl.loop(1, groups)
         def _(k):
@@ -572,7 +564,16 @@
 
             @pl.when(dest < kept)
             def _():
-                q_copy(comp, dest, me).wait_send()
+                q_copy(batch, dest, me).wait_send()
+
+
+def store_kernel(next_ref, div_ref, next_out, div_out, sem):
+    copies = [pltpu.make_async_copy(next_ref.at[f], next_out.at[f], sem.at[f]) for f in range(3)]
+    copies.append(pltpu.make_async_copy(div_ref, div_out, sem.at[3]))
+    for copy in copies:
+        copy.start()
+    for copy in copies:
+        copy.wait()
 
 
 def in_one_kernel(velocity, mode_mask):
@@ -588,41 +589,47 @@
     operands = [velocity, mode_mask] + [jnp.asarray(t) for t in tables(ncols, nrows, lines)]
     operands.append(jnp.asarray(kx))
     f32 = jnp.float32
+    hbm = pl.BlockSpec(memory_space=pltpu.HBM)
     whole = pl.BlockSpec(memory_space=pl.ANY)
+    vmem = pl.BlockSpec(memory_space=pltpu.VMEM)
     dma = pltpu.SemaphoreType.DMA
-    change, divergence = pl.pallas_call(
+    shapes = (
+        jax.ShapeDtypeStruct(velocity.shape, f32),
+        jax.ShapeDtypeStruct(velocity.shape[1:], f32),
+    )
+    following, divergence = pl.pallas_call(
         functools.partial(kernel, groups, kept),
-        out_shape=(
-            jax.ShapeDtypeStruct(velocity.shape, f32),
-            jax.ShapeDtypeStruct(velocity.shape[1:], f32),
-        ),
-        in_specs=[pl.BlockSpec(memory_space=pltpu.HBM)] * len(operands),
-        out_specs=(whole, whole),
+        out_shape=shapes,
+        in_specs=[hbm] * len(operands),
+        out_specs=(vmem, vmem),
         scratch_shapes=[pltpu.VMEM(t.shape, t.dtype) for t in operands]
         + [
-            pltpu.VMEM(velocity.shape, f32),
-            pltpu.VMEM(velocity.shape[1:], f32),
-            pltpu.VMEM((5, groups, kyl, LANES), f32),
-            pltpu.VMEM((5, groups, kyl, LANES), f32),
+            pltpu.VMEM((groups, 5, kyl, LANES), f32),
+            pltpu.VMEM((groups, 5, kyl, LANES), f32),
             pltpu.VMEM((3, 2, kyl, ncols), f32),
             pltpu.VMEM((groups, kyl, LANES), f32),
-            pltpu.VMEM((3, groups, kyl, LANES), f32),
-            pltpu.VMEM((3, groups, kyl, LANES), f32),
+            pltpu.VMEM((groups, 3, kyl, LANES), f32),
+            pltpu.VMEM((groups, 3, kyl, LANES), f32),
             pltpu.VMEM((2, kyl, ncols), f32),
             pltpu.VMEM((3, 4, half // 2, LANES), f32),
             dma((10,)),
-            dma((4,)),
-            dma((5, groups)),
-            dma((5, groups)),
-            dma((3, groups)),
-            dma((3, groups)),
-            dma((8,)),
+            dma((len(field_batches), groups)),
+            dma((len(field_batches), groups)),
+            dma((len(back_batches), groups)),
+            dma((len(back_batches), groups)),
             dma((5,)),
             dma((5,)),
         ],
         compiler_params=pltpu.CompilerParams(collective_id=0, has_side_effects=True, vmem_limit_bytes=32 * 2**20),
     )(*[pltpu.with_memory_space_constraint(x, pltpu.HBM) for x in operands])
-    return velocity + change, divergence
+    return pl.pallas_call(
+        store_kernel,
+        out_shape=shapes,
+        in_specs=[whole, whole],
+        out_specs=(hbm, hbm),
+        scratch_shapes=[dma((4,))],
+        compiler_params=pltpu.CompilerParams(vmem_limit_bytes=2**20),
+    )(following, divergence)
 
 
 def on_device(velocity, mode_mask):

time: 60.1 us -> 55.4 us (0.922)
  the two profiles are of different devices: /device:TPU:0 before, /device:TPU:8 now
where the time goes in v1:
time: 55.4 us; the launch traced here: 55.1 us
  Pallas kernels  54.5 us (98%)
  between operations  0.64 us (1%)
    pallas_call x1, Pallas kernels, in_one_kernel(): pl.pallas_call(functools.partial(kernel, groups, kept), out_shape=shapes,...  53.5 us

profile of v1, /device:TPU:8, one launch (start us, length us, event | category | flops | bytes accessed | tf_op | source)
XLA Modules:
  0.0 55.1 jit_solution(14051709471202047936)
XLA Ops:
  0.6 53.5 %shard_map.95 = (f32[3,1,2,32,1024]{4,3,2,1,0:T(8,128)S(1)}, f32[1,2,32,1024]{3,2,1,0:T(8,128)S(1)}) custom-call(f32[3,1,2,32,1024]{4,3,2,1,0:T(8,128)} %vel_hbm.1, s32[32,1024]{1,0:T(8,128)} %mask_hbm.1, f32[256,256]{1,0:T(8,128)} %constant.12.clone.to_grid_hbm, f32[256,256]{1,0:T(8,128)} %constant.13.clone.to_wave_hbm, ...), custom_call_target="tpu_custom_call" | custom-call | tf_op jit(solution)/shard_map/pallas_call | solution.py:600
  54.1 1.0 %shard_map.96 = (f32[3,1,2,32,1024]{4,3,2,1,0:T(8,128)}, f32[1,2,32,1024]{3,2,1,0:T(8,128)}) custom-call(f32[3,1,2,32,1024]{4,3,2,1,0:T(8,128)S(1)} %get-tuple-element.4.next_ref, f32[1,2,32,1024]{3,2,1,0:T(8,128)S(1)} %get-tuple-element.5.div_ref), custom_call_target="tpu_custom_call" | custom-call | tf_op jit(solution)/shard_map/pallas_call | solution.py:625

commit v2 on v1

--- a/solution.py
+++ b/solution.py
@@ -232,6 +232,8 @@
     return [np.asarray(t, np.float32) for t in (to_grid, to_wave, span, span_turn, line_turn)]
 
 
+PLANE = 4
+NEAR = 1
 field_batches = ((0, 2), (2, 2), (4, 1))
 back_batches = ((0, 1), (1, 2))
 
@@ -242,7 +244,8 @@
     out, div,
     vel, mask, to_grid, to_wave, span, span_turn, line_turn, kx_ref,
     send, recv, vel_other, g_other, q_send, q_recv, w_other, grid,
-    load_sem, send_sem, recv_sem, q_send_sem, q_recv_sem, pair_sem, pair_recv_sem,
+    load_sem, send_sem, recv_sem, q_send_sem, q_recv_sem, pair_sem, pair_recv_sem, ready,
+    hop, hop_sem, hop_recv_sem, pass_sem,
 ):
     me = lax.axis_index("pa")
     side = lax.axis_index("gz")
@@ -255,6 +258,45 @@
     quarter = half // 2
     radix = ncols // LANES
     dz = jnp.where(side == 0, 0.5, -0.5).astype(jnp.float32)
+
+    depth = groups // PLANE
+    diameter = depth + 1
+    layer = me // PLANE
+    column = lax.rem(me, PLANE)
+    flipped = [column]
+    for step in (1, 2):
+        flipped += [f + step - 2 * step * lax.rem(f // step, 2) for f in flipped]
+    reach = sorted(range(1 - depth, depth), key=lambda d: (-abs(d), -d))
+
+    def columns_within(shift, low, high):
+        return [c for c in range(PLANE) if low <= abs(shift) + c.bit_count() <= high]
+
+    def each_peer(low, high, act):
+        for shift in reach:
+            chosen = columns_within(shift, low, high)
+            if not chosen:
+                continue
+
+            def visit(shift=shift, chosen=chosen):
+                for c in chosen:
+                    act((layer + shift) * PLANE + flipped[c])
+
+            if shift == 0:
+                visit()
+            else:
+                pl.when((layer + shift >= 0) & (layer + shift < depth))(visit)
+
+    def peers(low, high):
+        total = 0
+        for shift in reach:
+            count = len(columns_within(shift, low, high))
+            inside = (layer + shift >= 0) & (layer + shift < depth)
+            total = total + jnp.where(inside, count, 0)
+        return total
+
+    barrier = pltpu.get_barrier_semaphore()
+    each_peer(1, NEAR, lambda d: pl.semaphore_signal(barrier, inc=1, device_id={"pa": d}))
+    pl.semaphore_signal(barrier, inc=1, device_id=partner)
 
     loads = {}
     for index, (name, src, dst) in enumerate(
@@ -274,14 +316,6 @@
         loads[name] = pltpu.make_async_copy(src, dst, load_sem.at[index])
         loads[name].start()
 
-    barrier = pltpu.get_barrier_semaphore()
-
-    @pl.loop(1, groups)
-    def _(k):
-        pl.semaphore_signal(barrier, inc=1, device_id={"pa": lax.rem(me + k, groups)})
-
-    pl.semaphore_signal(barrier, inc=1, device_id=partner)
-
     own_n = me * kyl + lax.broadcasted_iota(jnp.int32, (kyl, LANES), 0)
     ky_own = 2.0 * math.pi / nrows * own_n.astype(jnp.float32)
     weight = jnp.where(own_n == 0, 0.5, 1.0).astype(jnp.float32)
@@ -330,6 +364,9 @@
         def _(k):
             batch_copy(batch, lax.rem(me + k, groups), me).start()
 
+        keep_own(batch)
+
+    def keep_own(batch):
         first_slot, count = field_batches[batch]
         for slot in range(first_slot, first_slot + count):
             recv[me, slot] = send[me, slot]
@@ -338,7 +375,10 @@
         @pl.loop(1, groups)
         def _(k):
             source = lax.rem(me + groups - k, groups)
-            batch_copy(batch, source, source).wait_recv()
+
+            @pl.when((source != mate) | jnp.logical_not(middle) | (batch > 0))
+            def _():
+                batch_copy(batch, source, source).wait_recv()
 
     def pair_copy(index, src, dst):
         return pltpu.make_async_remote_copy(
@@ -354,12 +394,88 @@
     x_forward(1, [spec(0, a) for a in range(radix)])
     loads["w"].wait()
     loads["kx"].wait()
-    pl.semaphore_wait(barrier, groups)
-    send_batch(0)
+    pl.semaphore_wait(barrier, peers(1, NEAR) + 1)
+
+    half_depth = depth // 2
+    upper = layer >= half_depth
+    middle = (layer == half_depth) | (layer == half_depth - 1)
+    mate = jnp.where(upper, me - PLANE, me + PLANE)
+    own_half = jnp.where(upper, groups // 2, 0)
+    other_half = groups // 2 - own_half
+    lead = pl.ds(*field_batches[0])
+
+    def hop_copy(index):
+        return pltpu.make_async_remote_copy(
+            src_ref=send.at[pl.ds(other_half + index * PLANE, PLANE), lead],
+            dst_ref=hop.at[index],
+            send_sem=hop_sem.at[index],
+            recv_sem=hop_recv_sem.at[index],
+            device_id={"pa": mate},
+        )
+
+    def pass_copy(index, c):
+        return pltpu.make_async_remote_copy(
+            src_ref=hop.at[index, c],
+            dst_ref=recv.at[mate, lead],
+            send_sem=pass_sem.at[index, c],
+            recv_sem=recv_sem.at[0, mate],
+            device_id={"pa": own_half + index * PLANE + c},
+        )
+
+    def each_pass(index, act):
+        for c in range(PLANE):
+
+            @pl.when(own_half + index * PLANE + c != me)
+            def _():
+                act(pass_copy(index, c))
+
+    def pass_on():
+        @pl.when(middle)
+        def _():
+            for index in range(half_depth):
+                hop_copy(index).wait_recv()
+                each_pass(index, lambda copy: copy.start())
+                for c in range(PLANE):
+
+                    @pl.when(own_half + index * PLANE + c == me)
+                    def _():
+                        recv[mate, lead] = hop[index, c]
+
+    def direct(dest):
+        return jnp.logical_not(middle & ((dest >= groups // 2) != upper))
+
+    steps = []
+    known = NEAR
+    while known < diameter:
+        steps.append(min(known, diameter - known))
+        known += steps[-1]
+
+    def tell(index):
+        if index < len(steps):
+            each_peer(
+                1,
+                steps[index],
+                lambda d: pl.semaphore_signal(ready.at[index], inc=1, device_id={"pa": d}),
+            )
+
+    def hear(index):
+        if index < len(steps):
+            pl.semaphore_wait(ready.at[index], peers(1, steps[index]))
+            tell(index + 1)
+
+    tell(0)
+
+    @pl.when(middle)
+    def _():
+        for index in range(half_depth):
+            hop_copy(index).start()
+
+    keep_own(0)
     vel_copies = [pair_copy(f, vel.at[f, 0], vel_other.at[f]) for f in range(3)]
     for copy in vel_copies:
         copy.start()
     x_forward(2, [spec(2, a) for a in range(radix)])
+    hear(0)
     vel_copies[0].wait_recv()
     swirl = []
     for a in range(radix):
@@ -367,6 +483,17 @@
         at = slice(a * LANES, (a + 1) * LANES)
         swirl.append((dz * vel_other[0, 0, :, at] + kx * w[1], dz * vel_other[0, 1, :, at] - kx * w[0]))
     x_forward(3, swirl)
+    for index in range(1, len(steps)):
+        hear(index)
+
+    @pl.loop(1, groups)
+    def _(k):
+        dest = lax.rem(me + k, groups)
+
+        @pl.when(direct(dest))
+        def _():
+            batch_copy(0, dest, me).start()
+
     send_batch(1)
     swirl = []
     for a in range(radix):
@@ -476,6 +603,7 @@
             for comp, value in zip(comps, packed):
                 q_send[base : base + count, comp] = value[: count * kyl].reshape(count, kyl, LANES)
 
+    pass_on()
     wait_batch(0)
     v_copy = pair_copy(3, recv.at[:, 0], g_other)
     v_copy.start()
@@ -550,11 +678,21 @@
     for copy in vel_copies + [v_copy, w_copy]:
         copy.wait_send()
 
+    @pl.when(middle)
+    def _():
+        for index in range(half_depth):
+            hop_copy(index).wait_send()
+            each_pass(index, lambda copy: copy.wait_send())
+
     for batch in range(len(field_batches)):
 
         @pl.loop(1, groups)
         def _(k):
-            batch_copy(batch, lax.rem(me + k, groups), me).wait_send()
+            dest = lax.rem(me + k, groups)
+
+            @pl.when(direct(dest) | (batch > 0))
+            def _():
+                batch_copy(batch, dest, me).wait_send()
 
     for batch in range(len(back_batches)):
 
@@ -589,6 +727,7 @@
     operands = [velocity, mode_mask] + [jnp.asarray(t) for t in tables(ncols, nrows, lines)]
     operands.append(jnp.asarray(kx))
     f32 = jnp.float32
+    halves = groups // PLANE // 2
     hbm = pl.BlockSpec(memory_space=pltpu.HBM)
     whole = pl.BlockSpec(memory_space=pl.ANY)
     vmem = pl.BlockSpec(memory_space=pltpu.VMEM)
@@ -619,6 +758,11 @@
             dma((len(back_batches), groups)),
             dma((5,)),
             dma((5,)),
+            pltpu.SemaphoreType.REGULAR((groups,)),
+            pltpu.VMEM((halves, PLANE, field_batches[0][1], kyl, LANES), f32),
+            dma((halves,)),
+            dma((halves,)),
+            dma((halves, PLANE)),
         ],
         compiler_params=pltpu.CompilerParams(collective_id=0, has_side_effects=True, vmem_limit_bytes=32 * 2**20),
     )(*[pltpu.with_memory_space_constraint(x, pltpu.HBM) for x in operands])
@@ -640,6 +784,7 @@
         lax.axis_size("gz") == 2
         and velocity.shape[1] == 1
         and kyl % 8 == 0
+        and groups % (2 * PLANE) == 0
         and 2 * (ncols // groups) == LANES
         and (kyl * groups // 2) % LANES == 0
         and ncols % LANES == 0

time: 55.4 us -> 54.7 us (0.987)
  no operation moved by 1% of the time
where the time goes in v2:
time: 54.7 us; the launch traced here: 54.6 us
  Pallas kernels  54 us (99%)
  between operations  0.64 us (1%)
    pallas_call x1, Pallas kernels, in_one_kernel(): pl.pallas_call(functools.partial(kernel, groups, kept), out_shape=shapes,...  53 us

profile of v2, /device:TPU:8, one launch (start us, length us, event | category | flops | bytes accessed | tf_op | source)
XLA Modules:
  0.0 54.6 jit_solution(18182466056855109484)
XLA Ops:
  0.6 53.0 %shard_map.95 = (f32[3,1,2,32,1024]{4,3,2,1,0:T(8,128)S(1)}, f32[1,2,32,1024]{3,2,1,0:T(8,128)S(1)}) custom-call(f32[3,1,2,32,1024]{4,3,2,1,0:T(8,128)} %vel_hbm.1, s32[32,1024]{1,0:T(8,128)} %mask_hbm.1, f32[256,256]{1,0:T(8,128)} %constant.12.clone.to_grid_hbm, f32[256,256]{1,0:T(8,128)} %constant.13.clone.to_wave_hbm, ...), custom_call_target="tpu_custom_call" | custom-call | tf_op jit(solution)/shard_map/pallas_call | solution.py:739
  53.6 1.0 %shard_map.96 = (f32[3,1,2,32,1024]{4,3,2,1,0:T(8,128)}, f32[1,2,32,1024]{3,2,1,0:T(8,128)}) custom-call(f32[3,1,2,32,1024]{4,3,2,1,0:T(8,128)S(1)} %get-tuple-element.4.next_ref, f32[1,2,32,1024]{3,2,1,0:T(8,128)S(1)} %get-tuple-element.5.div_ref), custom_call_target="tpu_custom_call" | custom-call | tf_op jit(solution)/shard_map/pallas_call | solution.py:769

commit v3 on v2

--- a/solution.py
+++ b/solution.py
@@ -390,10 +390,6 @@
         )
 
     x_forward(0, [spec(1, a) for a in range(radix)])
-    loads["u"].wait()
-    x_forward(1, [spec(0, a) for a in range(radix)])
-    loads["w"].wait()
-    loads["kx"].wait()
     pl.semaphore_wait(barrier, peers(1, NEAR) + 1)
 
     half_depth = depth // 2
@@ -404,14 +400,20 @@
     other_half = groups // 2 - own_half
     lead = pl.ds(*field_batches[0])
 
-    def hop_copy(index):
+    def hop_copy(index, slot):
         return pltpu.make_async_remote_copy(
-            src_ref=send.at[pl.ds(other_half + index * PLANE, PLANE), lead],
-            dst_ref=hop.at[index],
-            send_sem=hop_sem.at[index],
-            recv_sem=hop_recv_sem.at[index],
+            src_ref=send.at[pl.ds(other_half + index * PLANE, PLANE), slot],
+            dst_ref=hop.at[index, :, slot],
+            send_sem=hop_sem.at[index, slot],
+            recv_sem=hop_recv_sem.at[index, slot],
             device_id={"pa": mate},
         )
+
+    def send_hops(slot):
+        @pl.when(middle)
+        def _():
+            for index in range(half_depth):
+                hop_copy(index, slot).start()
 
     def pass_copy(index, c):
         return pltpu.make_async_remote_copy(
@@ -433,7 +435,8 @@
         @pl.when(middle)
         def _():
             for index in range(half_depth):
-                hop_copy(index).wait_recv()
+                for slot in range(field_batches[0][1]):
+                    hop_copy(index, slot).wait_recv()
                 each_pass(index, lambda copy: copy.start())
                 for c in range(PLANE):
 
@@ -465,11 +468,12 @@
 
     tell(0)
 
-    @pl.when(middle)
-    def _():
-        for index in range(half_depth):
-            hop_copy(index).start()
-
+    send_hops(0)
+    loads["u"].wait()
+    x_forward(1, [spec(0, a) for a in range(radix)])
+    send_hops(1)
+    loads["w"].wait()
+    loads["kx"].wait()
     keep_own(0)
     vel_copies = [pair_copy(f, vel.at[f, 0], vel_other.at[f]) for f in range(3)]
     for copy in vel_copies:
@@ -575,11 +579,12 @@
         for slot in range(first_slot, first_slot + count):
             q_recv[me, slot] = q_send[me, slot]
 
-    def q_wait(batch):
-        @pl.loop(1, groups)
-        def _(k):
-            source = lax.rem(me + groups - k, groups)
-            q_copy(batch, source, source).wait_recv()
+    def q_wait(batch, first_source, last_source):
+        @pl.loop(first_source, last_source)
+        def _(source):
+            @pl.when(source != me)
+            def _():
+                q_copy(batch, source, source).wait_recv()
 
     def y_back(columns, comps):
         res = dot3(back_w, split(jnp.concatenate(columns, 1)))
@@ -633,16 +638,18 @@
     loads["mask"].wait()
     wave_w = split(to_wave[...])
 
-    def x_back(slot, comp):
+    def x_lines(slot, residues):
         rows = [
-            jnp.concatenate([q_recv[2 * c, slot], q_recv[2 * c + 1, slot]], 1)
-            for c in range(radix)
+            jnp.concatenate([q_recv[2 * c, slot], q_recv[2 * c + 1, slot]], 1) for c in residues
         ]
         res = dot3(split(jnp.concatenate(rows, 0)), wave_w)
+        return [res[j * kyl : (j + 1) * kyl] for j in range(len(residues))]
+
+    def x_back(comp, lines_of):
         z = []
         for c in range(radix):
-            r = res[c * kyl : (c + 1) * kyl, :LANES]
-            i = res[c * kyl : (c + 1) * kyl, LANES:]
+            r = lines_of[c][:, :LANES]
+            i = lines_of[c][:, LANES:]
             if c > 0:
                 tc = jnp.broadcast_to(line_turn[c : c + 1, :], (kyl, LANES))
                 ts = jnp.broadcast_to(line_turn[radix + c : radix + c + 1, :], (kyl, LANES))
@@ -656,17 +663,50 @@
 
     @pl.when(me < kept)
     def _():
-        q_wait(0)
-        x_back(0, 2)
+        q_wait(0, 0, groups)
+        x_back(2, x_lines(0, range(radix)))
 
     w_copy = pair_copy(4, out.at[2, 0], w_other)
     w_copy.start()
 
+    for copy in vel_copies + [v_copy]:
+        copy.wait_send()
+
+    @pl.when(middle)
+    def _():
+        for index in range(half_depth):
+            for slot in range(field_batches[0][1]):
+                hop_copy(index, slot).wait_send()
+            each_pass(index, lambda copy: copy.wait_send())
+
+    for batch in range(len(field_batches)):
+
+        @pl.loop(1, groups)
+        def _(k):
+            dest = lax.rem(me + k, groups)
+
+            @pl.when(direct(dest) | (batch > 0))
+            def _():
+                batch_copy(batch, dest, me).wait_send()
+
+    for batch in range(len(back_batches)):
+
+        @pl.loop(1, groups)
+        def _(k):
+            dest = lax.rem(me + k, groups)
+
+            @pl.when(dest < kept)
+            def _():
+                q_copy(batch, dest, me).wait_send()
+
     @pl.when(me < kept)
     def _():
-        q_wait(1)
-        x_back(1, 0)
-        x_back(2, 1)
+        half_radix = radix // 2
+        q_wait(1, 0, groups // 2)
+        near = [x_lines(slot, range(half_radix)) for slot in (1, 2)]
+        q_wait(1, groups // 2, groups)
+        for slot in (1, 2):
+            x_back(slot - 1, near[slot - 1] + x_lines(slot, range(half_radix, radix)))
 
     kx_all = kx_ref[...]
     w_copy.wait_recv()
@@ -675,39 +715,18 @@
         v_next = out[1, 0, 1 - part]
         div[0, part] = dz * w_other[part] + sign * (kx_all * u_next + ky_wide * v_next)
 
-    for copy in vel_copies + [v_copy, w_copy]:
-        copy.wait_send()
-
-    @pl.when(middle)
-    def _():
-        for index in range(half_depth):
-            hop_copy(index).wait_send()
-            each_pass(index, lambda copy: copy.wait_send())
-
-    for batch in range(len(field_batches)):
-
-        @pl.loop(1, groups)
-        def _(k):
-            dest = lax.rem(me + k, groups)
-
-            @pl.when(direct(dest) | (batch > 0))
-            def _():
-                batch_copy(batch, dest, me).wait_send()
-
-    for batch in range(len(back_batches)):
-
-        @pl.loop(1, groups)
-        def _(k):
-            dest = lax.rem(me + k, groups)
-
-            @pl.when(dest < kept)
-            def _():
-                q_copy(batch, dest, me).wait_send()
+    w_copy.wait_send()
 
 
 def store_kernel(next_ref, div_ref, next_out, div_out, sem):
-    copies = [pltpu.make_async_copy(next_ref.at[f], next_out.at[f], sem.at[f]) for f in range(3)]
-    copies.append(pltpu.make_async_copy(div_ref, div_out, sem.at[3]))
+    copies = [
+        pltpu.make_async_copy(next_ref.at[f, 0, p], next_out.at[f, 0, p], sem.at[2 * f + p])
+        for f in range(3)
+        for p in range(2)
+    ]
+    copies += [
+        pltpu.make_async_copy(div_ref.at[0, p], div_out.at[0, p], sem.at[6 + p]) for p in range(2)
+    ]
     for copy in copies:
         copy.start()
     for copy in copies:
@@ -760,8 +779,8 @@
             dma((5,)),
             pltpu.SemaphoreType.REGULAR((groups,)),
             pltpu.VMEM((halves, PLANE, field_batches[0][1], kyl, LANES), f32),
-            dma((halves,)),
-            dma((halves,)),
+            dma((halves, field_batches[0][1])),
+            dma((halves, field_batches[0][1])),
             dma((halves, PLANE)),
         ],
         compiler_params=pltpu.CompilerParams(collective_id=0, has_side_effects=True, vmem_limit_bytes=32 * 2**20),
@@ -771,7 +790,7 @@
         out_shape=shapes,
         in_specs=[whole, whole],
         out_specs=(hbm, hbm),
-        scratch_shapes=[dma((4,))],
+        scratch_shapes=[dma((8,))],
         compiler_params=pltpu.CompilerParams(vmem_limit_bytes=2**20),
     )(following, divergence)
 

time: 54.7 us -> 53.6 us (0.980)
  Pallas kernels: 54 us -> 52.9 us
    pallas_call x1, Pallas kernels: 53 us -> 51.8 us  [in_one_kernel(): pl.pallas_call(functools.partial(kernel, groups, kept), out_shape=shapes,...]
where the time goes in v3:
time: 53.6 us; the launch traced here: 53.5 us
  Pallas kernels  52.9 us (99%)
  between operations  0.64 us (1%)
    pallas_call x1, Pallas kernels, in_one_kernel(): pl.pallas_call(functools.partial(kernel, groups, kept), out_shape=shapes,...  51.8 us

profile of v3, /device:TPU:8, one launch (start us, length us, event | category | flops | bytes accessed | tf_op | source)
XLA Modules:
  0.0 53.5 jit_solution(3225875105600968241)
XLA Ops:
  0.6 51.8 %shard_map.95 = (f32[3,1,2,32,1024]{4,3,2,1,0:T(8,128)S(1)}, f32[1,2,32,1024]{3,2,1,0:T(8,128)S(1)}) custom-call(f32[3,1,2,32,1024]{4,3,2,1,0:T(8,128)} %vel_hbm.1, s32[32,1024]{1,0:T(8,128)} %mask_hbm.1, f32[256,256]{1,0:T(8,128)} %constant.12.clone.to_grid_hbm, f32[256,256]{1,0:T(8,128)} %constant.13.clone.to_wave_hbm, ...), custom_call_target="tpu_custom_call" | custom-call | tf_op jit(solution)/shard_map/pallas_call | solution.py:758
  52.5 1.0 %shard_map.96 = (f32[3,1,2,32,1024]{4,3,2,1,0:T(8,128)}, f32[1,2,32,1024]{3,2,1,0:T(8,128)}) custom-call(f32[3,1,2,32,1024]{4,3,2,1,0:T(8,128)S(1)} %get-tuple-element.4.next_ref, f32[1,2,32,1024]{3,2,1,0:T(8,128)S(1)} %get-tuple-element.5.div_ref), custom_call_target="tpu_custom_call" | custom-call | tf_op jit(solution)/shard_map/pallas_call | solution.py:788

commit v4 on v3

--- a/solution.py
+++ b/solution.py
@@ -466,9 +466,8 @@
             pl.semaphore_wait(ready.at[index], peers(1, steps[index]))
             tell(index + 1)
 
+    send_hops(0)
     tell(0)
-
-    send_hops(0)
     loads["u"].wait()
     x_forward(1, [spec(0, a) for a in range(radix)])
     send_hops(1)
@@ -669,7 +668,7 @@
     w_copy = pair_copy(4, out.at[2, 0], w_other)
     w_copy.start()
 
-    for copy in vel_copies + [v_copy]:
+    for copy in vel_copies + [v_copy, w_copy]:
         copy.wait_send()
 
     @pl.when(middle)
@@ -698,6 +697,8 @@
             @pl.when(dest < kept)
             def _():
                 q_copy(batch, dest, me).wait_send()
+
+    w_copy.wait_recv()
 
     @pl.when(me < kept)
     def _():
@@ -709,13 +710,10 @@
             x_back(slot - 1, near[slot - 1] + x_lines(slot, range(half_radix, radix)))
 
     kx_all = kx_ref[...]
-    w_copy.wait_recv()
     for part, sign in ((0, -1.0), (1, 1.0)):
         u_next = out[0, 0, 1 - part]
         v_next = out[1, 0, 1 - part]
         div[0, part] = dz * w_other[part] + sign * (kx_all * u_next + ky_wide * v_next)
-
-    w_copy.wait_send()
 
 
 def store_kernel(next_ref, div_ref, next_out, div_out, sem):

time: 53.6 us -> 53.6 us (level)
  no operation moved by 1% of the time
where the time goes in v4:
time: 53.6 us; the launch traced here: 53.5 us
  Pallas kernels  52.9 us (99%)
  between operations  0.64 us (1%)
    pallas_call x1, Pallas kernels, in_one_kernel(): pl.pallas_call(functools.partial(kernel, groups, kept), out_shape=shapes,...  51.8 us

profile of v4, /device:TPU:8, one launch (start us, length us, event | category | flops | bytes accessed | tf_op | source)
XLA Modules:
  0.0 53.5 jit_solution(14810813843992466511)
XLA Ops:
  0.6 51.8 %shard_map.95 = (f32[3,1,2,32,1024]{4,3,2,1,0:T(8,128)S(1)}, f32[1,2,32,1024]{3,2,1,0:T(8,128)S(1)}) custom-call(f32[3,1,2,32,1024]{4,3,2,1,0:T(8,128)} %vel_hbm.1, s32[32,1024]{1,0:T(8,128)} %mask_hbm.1, f32[256,256]{1,0:T(8,128)} %constant.12.clone.to_grid_hbm, f32[256,256]{1,0:T(8,128)} %constant.13.clone.to_wave_hbm, ...), custom_call_target="tpu_custom_call" | custom-call | tf_op jit(solution)/shard_map/pallas_call | solution.py:756
  52.5 1.0 %shard_map.96 = (f32[3,1,2,32,1024]{4,3,2,1,0:T(8,128)}, f32[1,2,32,1024]{3,2,1,0:T(8,128)}) custom-call(f32[3,1,2,32,1024]{4,3,2,1,0:T(8,128)S(1)} %get-tuple-element.4.next_ref, f32[1,2,32,1024]{3,2,1,0:T(8,128)S(1)} %get-tuple-element.5.div_ref), custom_call_target="tpu_custom_call" | custom-call | tf_op jit(solution)/shard_map/pallas_call | solution.py:786
